TPU v7x, 32 devices: a whole 2x2x4 slice. The times are simulated.
32 devices in a mesh: span: 8 (over z, x), chord: 4 (over y, core).
Axes of the slice: x: 2, y: 2, z: 4, core: 2. Of those that a mesh axis runs over, the one named last changes fastest.
Arguments:
- fluid_state: float32 [4, 256, 128, 128], P(None, 'span', 'chord'), may hold values from -6 to 6
- shell_disp: float32 [3, 1024, 512], P(None, 'span', 'chord'), may hold values from -6 to 6
- shell_vel: float32 [3, 1024, 512], P(None, 'span', 'chord'), may hold values from -6 to 6
- owners: int32 [32768, 4], P(('span', 'chord')), may hold values from 0 to 31, all different within a row; in each aligned block of 1024 rows (0 to 1023, 1024 to 2047, ...) at most 256 rows name the same one
- node_local: int32 [32768, 4], P(('span', 'chord')), may hold values from 0 to 16383
- rbf_weight: float32 [32768, 4], P(('span', 'chord')), may hold values from 0.2 to 1
- normals: float32 [3, 32768], P(None, ('span', 'chord')), may hold values from -6 to 6
Outputs:
- fluid_next: float32 [4, 256, 128, 128], P(None, 'span', 'chord')
- interface_motion: float32 [6, 32768], P(None, ('span', 'chord'))
- disp_next: float32 [3, 1024, 512], P(None, 'span', 'chord')
- vel_next: float32 [3, 1024, 512], P(None, 'span', 'chord')
Inputs may be any that keep to these rules, and one draw needn't show every extreme that they name: Each interface point names 4 different owners; the points of one device name no owner more than 256 times, a bound that some block reaches.
All inputs are finite; a program needn't handle non-finite values.
Results may differ from a plain program's by a relative error of at most 0.00007.
Values sent between devices are 32-bit elements; how exact they have to be, the bound alone decides.
No kernel may reach another device: no remote copies, remote signals or barrier semaphores. Data moves between devices by JAX's collectives and lax.ppermute only.
A program may use at most 64 MiB of HBM per device.

v0:
```python
import jax
import jax.numpy as jnp
from jax import lax
from jax.sharding import PartitionSpec as P

flow_speed = 0.5
time_step = 0.4
stiffness = 0.5
damping = 0.2
shell_step = 0.3


def with_halo(value, sides, width):
    for axis, dim in sides:
        size, length = (lax.axis_size(axis), value.shape[dim])
        up = [(i, (i + 1) % size) for i in range(size - 1)]
        down = [(j, i) for i, j in up]
        last = lax.slice_in_dim(value, length - width, length, axis=dim)
        leading = lax.slice_in_dim(value, 0, width, axis=dim)
        before = lax.ppermute(last, axis, up)
        after = lax.ppermute(leading, axis, down)
        value = jnp.concatenate([before, value, after], axis=dim)
    return value


def central(padded, direction):
    length = padded.shape[direction] - 6

    def window(offset):
        return lax.slice_in_dim(padded, 3 + offset, 3 + offset + length, axis=direction)

    return (
        45.0 * (window(1) - window(-1)) - 9.0 * (window(2) - window(-2)) + (window(3) - window(-3))
    ) / 60.0


def stencil_coef(distance):
    size = jnp.abs(distance)
    value = jnp.where(size == 1, 45.0, jnp.where(size == 2, -9.0, jnp.where(size == 3, 1.0, 0.0)))
    return value * jnp.sign(distance).astype(jnp.float32) / 60.0


def normal_tables(length):
    source = lax.broadcasted_iota(jnp.int32, (length, length), 0)
    target = lax.broadcasted_iota(jnp.int32, (length, length), 1)
    inner = stencil_coef(source - target)
    ghost = jnp.where(source < 3, stencil_coef(-(source + 1 + target)), 0.0)
    pressure_table = inner + ghost
    normal_table = inner - ghost
    wall_row = 2.0 * jnp.sum(ghost, axis=0)
    return (pressure_table, normal_table, wall_row)


def normal_derivatives(fluid, wall_motion):
    cells_x, cells_y, length = (fluid.shape[1], fluid.shape[2], fluid.shape[3])
    pressure_table, normal_table, wall_row = normal_tables(length)
    pressure_flat = fluid[0].reshape(cells_x * cells_y, length)
    normal_flat = fluid[3].reshape(cells_x * cells_y, length)
    dz_pressure = jnp.dot(
        pressure_flat,
        pressure_table,
        precision=lax.Precision.HIGHEST,
        preferred_element_type=jnp.float32,
    )
    dz_normal = jnp.dot(
        normal_flat,
        normal_table,
        precision=lax.Precision.HIGHEST,
        preferred_element_type=jnp.float32,
    )
    dz_normal = dz_normal + wall_motion[2].reshape(-1)[:, None] * wall_row[None, :]
    return (
        dz_pressure.reshape(cells_x, cells_y, length),
        dz_normal.reshape(cells_x, cells_y, length),
    )


def fluid_rates(span_padded, chord_padded, dz_pressure, dz_normal):
    along_span = central(span_padded, 1)
    along_chord = central(chord_padded, 2)
    rate_p = -flow_speed * along_span[0] - (along_span[1] + along_chord[1] + dz_normal)
    rate_u = -flow_speed * along_span[1] - along_span[0]
    rate_v = -flow_speed * along_span[2] - along_chord[0]
    rate_w = -flow_speed * along_span[3] - dz_pressure
    return jnp.stack([rate_p, rate_u, rate_v, rate_w])


def laplacian(padded):
    center = padded[:, 1:-1, 1:-1]
    return (
        padded[:, 2:, 1:-1]
        + padded[:, :-2, 1:-1]
        + padded[:, 1:-1, 2:]
        + padded[:, 1:-1, :-2]
        - 4.0 * center
    )


def body(fluid_state, shell_disp, shell_vel, owners, node_local, rbf_weight, normals):
    span_count = lax.axis_size("span")
    chord_count = lax.axis_size("chord")
    devices = span_count * chord_count
    points, stencil = owners.shape
    capacity = max(2, (2 * points * stencil + devices - 1) // devices)
    owner_ids = owners.reshape(-1)
    node_ids = node_local.reshape(-1)
    columns = jnp.arange(devices, dtype=jnp.int32)
    onehot = (owner_ids[:, None] == columns[None, :]).astype(jnp.int32)
    before = jnp.cumsum(onehot, axis=0) - onehot
    order_in = jnp.sum(before * onehot, axis=1)
    slot_index = owner_ids * capacity + order_in
    requests = jnp.zeros((devices * capacity,), jnp.int32).at[slot_index].set(node_ids)
    asked_nodes = lax.all_to_all(
        requests, ("span", "chord"), split_axis=0, concat_axis=0, tiled=True
    )
    rows_x, rows_y = (shell_disp.shape[1], shell_disp.shape[2])
    stacked = jnp.concatenate([shell_disp, shell_vel], axis=0).reshape(6, rows_x * rows_y)
    picked = jnp.take(stacked, asked_nodes, axis=1)
    replies = lax.all_to_all(picked, ("span", "chord"), split_axis=1, concat_axis=1, tiled=True)
    motion = jnp.take(replies, slot_index, axis=1).reshape(6, points, stencil)
    interface_motion = jnp.sum(motion * rbf_weight[None], axis=2)
    cells_x, cells_y = (fluid_state.shape[1], fluid_state.shape[2])
    wall_motion = interface_motion[3:].reshape(3, cells_x, cells_y)
    padded_all = with_halo(fluid_state, (("span", 1), ("chord", 2)), 3)
    span_padded = padded_all[:, :, 3:-3]
    chord_padded = padded_all[0::2, 3:-3]
    dz_pressure, dz_normal = normal_derivatives(fluid_state, wall_motion)
    fluid_next = fluid_state + time_step * fluid_rates(
        span_padded, chord_padded, dz_pressure, dz_normal
    )
    pressure = fluid_next[0, :, :, 0].reshape(-1)
    surface_load = normals * pressure[None]
    contrib = (surface_load[:, :, None] * rbf_weight[None]).reshape(3, -1)
    outgoing = jnp.zeros((3, devices * capacity), jnp.float32).at[:, slot_index].set(contrib)
    arrived = lax.all_to_all(outgoing, ("span", "chord"), split_axis=1, concat_axis=1, tiled=True)
    shell_force = (
        jnp.zeros((3, rows_x * rows_y), jnp.float32)
        .at[:, asked_nodes]
        .add(arrived)
        .reshape(3, rows_x, rows_y)
    )
    shell_padded = with_halo(shell_disp, (("span", 1), ("chord", 2)), 1)
    bending = laplacian(shell_padded)
    acceleration = stiffness * bending + shell_force - damping * shell_vel
    vel_next = shell_vel + shell_step * acceleration
    disp_next = shell_disp + shell_step * vel_next
    return (fluid_next, interface_motion, disp_next, vel_next)


def solution(mesh):
    placed = (
        P(None, "span", "chord", None),
        P(None, "span", "chord"),
        P(None, "span", "chord"),
        P(("span", "chord"), None),
        P(("span", "chord"), None),
        P(("span", "chord"), None),
        P(None, ("span", "chord")),
    )
    return jax.shard_map(
        body,
        mesh=mesh,
        in_specs=placed,
        out_specs=(
            P(None, "span", "chord", None),
            P(None, ("span", "chord")),
            P(None, "span", "chord"),
            P(None, "span", "chord"),
        ),
        check_vma=False,
    )
```

profile of v0, /device:TPU:8, one launch (start us, length us, event | category | flops | bytes accessed | tf_op | source)
XLA Modules:
  0.0 256.4 jit_solution(6483146441333637341)
XLA Ops:
  1.4 0.9 copy.76
  3.5 9.2 %reduce-window.6 = s32[32,32,128]{2,1,0:T(8,128)S(1)} reduce-window(s32[32,32,128]{2,1,0:T(8,128)S(1)} %fusion.25, s32[]{:T(128)} %constant.34.clone.1), window={size=1x1x128 pad=0_0x0_0x127_0}, to_apply=%region_0.0 | reduce-window | flops 16646144 | bytes 1048580 | tf_op jit(solution)/shard_map/reduce-window
  12.7 0.8 slice_reduce_fusion.2
  14.9 16.1 %scatter_custom_fusion = s32[8192]{0:T(1024)} fusion(s32[4096]{0:T(1024)S(1)} %bitcast.73, s32[4096]{0:T(1024)S(1)} %reshape.173, s32[]{:T(128)} %constant.34.clone.1), kind=kCustom, calls=%fused_computation.117 | custom fusion | bytes 32772 | tf_op jit(solution)/shard_map/scatter | solution.py:112
  31.0 6.1 %all-to-all-start = ((s32[32,256,1]{1,2,0:T(1,128)}), s32[32,256,1]{1,2,0:T(1,128)}, u32[]{:S(2)}, u32[]{:S(2)}) async-start(s32[32,256,1]{1,2,0:T(1,128)} %bitcast.5), calls=%async_computation | async-start | bytes 65536 | tf_op jit(solution)/shard_map/all_to_all | solution.py:113
  37.1 0.8 fusion.91
  37.9 3.5 %collective-permute-start.1 = (f32[4,3,32,128]{3,2,1,0:T(8,128)}, f32[4,3,32,128]{3,2,1,0:T(8,128)}, u32[]{:S(2)}, u32[]{:S(2)}) collective-permute-start(f32[4,3,32,128]{3,2,1,0:T(8,128)} %get-tuple-element.34), channel_id=1, source_target_pairs={{0,4},{4,8},{8,12},{12,16},{16,20},{20,24},{24,28},{1,5},{5,9},{9,... | collective-permute-start | bytes 589832 | tf_op jit(solution)/shard_map/ppermute | solution.py:20
  41.4 3.4 %collective-permute-start = (f32[4,3,32,128]{3,2,1,0:T(8,128)}, f32[4,3,32,128]{3,2,1,0:T(8,128)}, u32[]{:S(2)}, u32[]{:S(2)}) collective-permute-start(f32[4,3,32,128]{3,2,1,0:T(8,128)} %get-tuple-element.33), channel_id=1, source_target_pairs={{4,0},{8,4},{12,8},{16,12},{20,16},{24,20},{28,24},{5,1},{9,5},{13... | collective-permute-start | bytes 589832 | tf_op jit(solution)/shard_map/ppermute | solution.py:21
  45.3 3.1 %collective-permute-start.4 = (f32[3,1,128]{2,1,0:T(1,128)}, f32[3,1,128]{2,1,0:T(1,128)S(1)}, u32[]{:S(2)}, u32[]{:S(2)}) collective-permute-start(f32[3,1,128]{2,1,0:T(1,128)} %get-tuple-element.38), channel_id=1, source_target_pairs={{4,0},{8,4},{12,8},{16,12},{20,16},{24,20},{28,24},{5,1},{9,5},{13... | collective-permute-start | bytes 4616 | tf_op jit(solution)/shard_map/ppermute | solution.py:21
  48.4 2.7 %collective-permute-start.5 = (f32[3,1,128]{2,1,0:T(1,128)}, f32[3,1,128]{2,1,0:T(1,128)}, u32[]{:S(2)}, u32[]{:S(2)}) collective-permute-start(f32[3,1,128]{2,1,0:T(1,128)} %get-tuple-element.37), channel_id=1, source_target_pairs={{0,4},{4,8},{8,12},{12,16},{16,20},{20,24},{24,28},{1,5},{5,9},{9,... | collective-permute-start | bytes 4616 | tf_op jit(solution)/shard_map/ppermute | solution.py:20
  51.2 0.9 fusion.90
  52.7 1.2 reduce_sum.32
  54.7 0.8 copy.78
  55.5 0.8 compare_and_fusion.1
  57.0 4.7 %copy.82 = f32[6,128,128]{0,2,1:T(8,128)} copy(f32[6,128,128]{2,1,0:T(8,128)S(1)} %pad_maximum_fusion.1) | data formatting | bytes 786432 | tf_op jit(solution)/shard_map/concatenate | solution.py:117
  61.9 0.9 copy.79
  62.8 1.0 copy.87
  63.9 0.9 mul.202
  65.4 0.8 compare_select_fusion
  66.2 31.2 %gather_fusion = f32[8192,6]{1,0:T(8,128)} fusion(f32[6,16384]{0,1:T(8,128)} %bitcast.58, s32[8192]{0:T(1024)S(1)} %broadcast_clamp_fusion), kind=kCustom, calls=%fused_computation | custom fusion | bytes 425984 | tf_op jit(solution)/shard_map/jit(_take)/gather | solution.py:118
  97.5 2.8 %copy.83 = f32[6,32,256]{2,0,1:T(8,128)S(1)} copy(f32[6,32,256]{0,2,1:T(8,128)} %bitcast.61) | data formatting | bytes 393216 | tf_op jit(solution)/shard_map/jit(_take)/gather | solution.py:118
  100.3 0.8 compare_and_fusion
  101.9 4.9 %all-to-all-start.1 = ((f32[6,32,256]{2,0,1:T(8,128)}), f32[6,32,256]{2,0,1:T(8,128)S(1)}, u32[]{:S(2)}, u32[]{:S(2)}) async-start(f32[6,32,256]{2,0,1:T(8,128)} %broadcast_select_fusion), calls=%async_computation.1 | async-start | bytes 524288 | tf_op jit(solution)/shard_map/all_to_all | solution.py:119
  106.8 1.0 constant_dynamic-update-slice_fusion.6
  107.8 0.9 constant_dynamic-update-slice_fusion.5
  108.6 1.0 constant_dynamic-update-slice_fusion.4
  109.7 1.3 collective-permute-start.3
  111.0 3.2 %collective-permute-start.2 = (f32[4,38,3,128]{3,2,1,0:T(4,128)S(1)}, f32[4,38,3,128]{3,2,1,0:T(4,128)S(1)}, u32[]{:S(2)}, u32[]{:S(2)}) collective-permute-start(f32[4,38,3,128]{3,2,1,0:T(4,128)S(1)} %get-tuple-element.24), channel_id=1, source_target_pairs={{0,1},{1,2},{2,3},{4,5},{5,6},{6,7},{8,9},{9,10},{10,11},{12,13},{... | collective-permute-start | bytes 700424 | tf_op jit(solution)/shard_map/ppermute | solution.py:20
  114.3 1.9 fusion.3
  116.7 1.6 fusion.14
  118.3 2.6 %copy.84 = f32[6,32,256]{0,2,1:T(8,128)} copy(f32[6,32,256]{2,0,1:T(8,128)S(1)} %all-to-all-done.1) | data formatting | bytes 393216 | tf_op jit(solution)/shard_map/all_to_all | solution.py:119
  121.0 16.4 %gather_fusion.1 = f32[4096,6]{1,0:T(8,128)} fusion(f32[6,8192]{0,1:T(8,128)} %bitcast.60, s32[4096]{0:T(1024)S(1)} %copy-done.9), kind=kCustom, calls=%fused_computation.1 | custom fusion | bytes 212992 | tf_op jit(solution)/shard_map/jit(_take)/gather | solution.py:120
  137.4 7.5 %multiply_reduce_fusion = f32[6,1024]{0,1:T(8,128)S(1)} fusion(f32[6,1024,4]{0,2,1:T(4,128)} %bitcast.62, f32[1024,4]{1,0:T(8,128)S(1)} %copy.85, pred[1024,4]{1,0:T(8,128)(4,1)} %copy.79), kind=kLoop, calls=%fused_computation.22 | loop fusion | flops 67584 | bytes 143360 | tf_op jit(solution)/shard_map/reduce_sum | solution.py:121
  145.3 1.5 fusion.12
  146.8 2.0 copy.86
  148.9 2.5 fusion.24
  151.9 1.3 copy-done.1
  154.1 14.9 %scatter_custom_fusion.1 = f32[3,8192]{0,1:T(8,128)} fusion(s32[4096]{0:T(1024)} %bitcast.75, f32[3,4096]{0,1:T(8,128)S(1)} %bitcast.59, f32[]{:T(128)} %constant.32.clone.1, f32[4096]{0:T(1024)} %mul.202), kind=kCustom, calls=%fused_computation.18 | custom fusion | flops 12288 | bytes 164352 | tf_op jit(solution)/shard_map/scatter | solution.py:134
  169.0 3.5 %copy.90 = f32[3,32,256]{2,0,1:T(4,128)} copy(f32[3,32,256]{0,2,1:T(8,128)} %bitcast.57) | data formatting | bytes 196608 | tf_op jit(solution)/shard_map/all_to_all | solution.py:135
  172.4 9.8 %all-to-all-start.2 = ((f32[3,32,256]{2,0,1:T(4,128)}), f32[3,32,256]{2,0,1:T(4,128)S(1)}, u32[]{:S(2)}, u32[]{:S(2)}) async-start(f32[3,32,256]{2,0,1:T(4,128)} %copy.90), calls=%async_computation.2 | async-start | bytes 262144 | tf_op jit(solution)/shard_map/all_to_all | solution.py:135
  182.4 2.0 collective-permute-start.7
  184.4 1.3 collective-permute-start.6
  185.7 0.8 copy.93
  186.5 2.8 %all-to-all-done.2 = f32[3,32,256]{2,0,1:T(4,128)S(1)} async-done(((f32[3,32,256]{2,0,1:T(4,128)}), f32[3,32,256]{2,0,1:T(4,128)S(1)}, u32[]{:S(2)}, u32[]{:S(2)}) %all-to-all-start.2) | async-done | bytes 98336 | tf_op jit(solution)/shard_map/all_to_all | solution.py:135
  189.3 2.6 %copy.91 = f32[8192,3]{1,0:T(8,128)} copy(f32[8192,3]{0,1:T(4,128)S(1)} %bitcast.68) | data formatting | bytes 196608 | tf_op jit(solution)/shard_map/all_to_all | solution.py:135
  191.9 57.3 %scatter_custom_fusion.2 = f32[3,16384]{0,1:T(8,128)} fusion(s32[8192]{0:T(1024)} %bitcast.71, f32[8192,3]{1,0:T(8,128)} %copy.91, f32[]{:T(128)} %constant.32.clone.1), kind=kCustom, calls=%fused_computation.5 | custom fusion | flops 24576 | bytes 197120 | tf_op jit(solution)/shard_map/scatter-add | solution.py:139
  249.3 5.3 %copy.92 = f32[3,128,128]{2,1,0:T(8,128)S(1)} copy(f32[3,128,128]{0,2,1:T(8,128)} %bitcast.56) | data formatting | bytes 393216 | tf_op jit(solution)/shard_map/reshape | solution.py:140
  254.6 1.8 multiply_add_fusion
  (82 shorter events, 10.1 us)
Async XLA Ops:
  2.6 11.3 %copy-start.11 = (s32[1024,4]{0,1:T(4,128)S(1)}, s32[1024,4]{0,1:T(4,128)}, u32[]{:S(2)}) copy-start(s32[1024,4]{0,1:T(4,128)} %param.11) | copy-start | bytes 49156
  3.5 33.6 %copy-start = (f32[4,32,32,128]{3,2,1,0:T(8,128)S(1)}, f32[4,32,32,128]{3,2,1,0:T(8,128)}, u32[]{:S(2)}) copy-start(f32[4,32,32,128]{3,2,1,0:T(8,128)} %param.7) | copy-start | bytes 6291460
  12.7 32.0 %copy-start.4 = (f32[3,128,128]{2,1,0:T(8,128)S(1)}, f32[3,128,128]{2,1,0:T(8,128)}, u32[]{:S(2)}) copy-start(f32[3,128,128]{2,1,0:T(8,128)} %param.8) | copy-start | bytes 589828
  14.8 22.3 %copy-start.7 = (s32[4096]{0:T(1024)}, s32[4096]{0:T(1024)S(1)}, u32[]{:S(2)}) copy-start(s32[4096]{0:T(1024)S(1)} %fusion.21) | copy-start | bytes 49156
  14.9 37.2 %copy-start.10 = (s32[4096,1]{0,1:T(1,128)}, s32[4096,1]{0,1:T(1,128)S(1)}, u32[]{:S(2)}) copy-start(s32[4096,1]{0,1:T(1,128)S(1)} %compare_select_fusion.1) | copy-start | bytes 49156
  31.0 34.5 %all-to-all-start = ((s32[32,256,1]{1,2,0:T(1,128)}), s32[32,256,1]{1,2,0:T(1,128)}, u32[]{:S(2)}, u32[]{:S(2)}) async-start(s32[32,256,1]{1,2,0:T(1,128)} %bitcast.5), calls=%async_computation | async-start | bytes 65536 | tf_op jit(solution)/shard_map/all_to_all | solution.py:113
  37.9 19.1 %copy-start.5 = (f32[3,128,128]{2,1,0:T(8,128)S(1)}, f32[3,128,128]{2,1,0:T(8,128)}, u32[]{:S(2)}) copy-start(f32[3,128,128]{2,1,0:T(8,128)} %param.9) | copy-start | bytes 589828
  37.9 68.9 %collective-permute-start.1 = (f32[4,3,32,128]{3,2,1,0:T(8,128)}, f32[4,3,32,128]{3,2,1,0:T(8,128)}, u32[]{:S(2)}, u32[]{:S(2)}) collective-permute-start(f32[4,3,32,128]{3,2,1,0:T(8,128)} %get-tuple-element.34), channel_id=1, source_target_pairs={{0,4},{4,8},{8,12},{12,16},{16,20},{20,24},{24,28},{1,5},{5,9},{9,... | collective-permute-start | bytes 589832 | tf_op jit(solution)/shard_map/ppermute | solution.py:20
  41.4 67.3 %collective-permute-start = (f32[4,3,32,128]{3,2,1,0:T(8,128)}, f32[4,3,32,128]{3,2,1,0:T(8,128)}, u32[]{:S(2)}, u32[]{:S(2)}) collective-permute-start(f32[4,3,32,128]{3,2,1,0:T(8,128)} %get-tuple-element.33), channel_id=1, source_target_pairs={{4,0},{8,4},{12,8},{16,12},{20,16},{24,20},{28,24},{5,1},{9,5},{13... | collective-permute-start | bytes 589832 | tf_op jit(solution)/shard_map/ppermute | solution.py:21
  45.3 19.4 %collective-permute-start.4 = (f32[3,1,128]{2,1,0:T(1,128)}, f32[3,1,128]{2,1,0:T(1,128)S(1)}, u32[]{:S(2)}, u32[]{:S(2)}) collective-permute-start(f32[3,1,128]{2,1,0:T(1,128)} %get-tuple-element.38), channel_id=1, source_target_pairs={{4,0},{8,4},{12,8},{16,12},{20,16},{24,20},{28,24},{5,1},{9,5},{13... | collective-permute-start | bytes 4616 | tf_op jit(solution)/shard_map/ppermute | solution.py:21
  48.4 16.3 %collective-permute-start.5 = (f32[3,1,128]{2,1,0:T(1,128)}, f32[3,1,128]{2,1,0:T(1,128)}, u32[]{:S(2)}, u32[]{:S(2)}) collective-permute-start(f32[3,1,128]{2,1,0:T(1,128)} %get-tuple-element.37), channel_id=1, source_target_pairs={{0,4},{4,8},{8,12},{12,16},{16,20},{20,24},{24,28},{1,5},{5,9},{9,... | collective-permute-start | bytes 4616 | tf_op jit(solution)/shard_map/ppermute | solution.py:20
  52.1 9.6 %copy-start.14 = (s32[128]{0:T(128)}, s32[128]{0:T(128)S(1)}, u32[]{:S(2)}) copy-start(s32[128]{0:T(128)S(1)} %iota_add_fusion.1) | copy-start | bytes 1540
  52.1 9.6 %copy-start.16 = (pred[128]{0:T(512)(128)(4,1)}, pred[128]{0:T(512)(128)(4,1)S(1)}, u32[]{:S(2)}) copy-start(pred[128]{0:T(512)(128)(4,1)S(1)} %iota_compare_fusion.2) | copy-start | bytes 388
  57.0 4.7 %copy-start.12 = (f32[1024,4]{0,1:T(4,128)S(1)}, f32[1024,4]{0,1:T(4,128)}, u32[]{:S(2)}) copy-start(f32[1024,4]{0,1:T(4,128)} %param.12) | copy-start | bytes 49156
  66.2 31.3 %copy-start.8 = (s32[8192,1]{0,1:T(1,128)}, s32[8192,1]{0,1:T(1,128)S(1)}, u32[]{:S(2)}) copy-start(s32[8192,1]{0,1:T(1,128)S(1)} %compare_select_fusion) | copy-start | bytes 98308
  101.9 16.5 %all-to-all-start.1 = ((f32[6,32,256]{2,0,1:T(8,128)}), f32[6,32,256]{2,0,1:T(8,128)S(1)}, u32[]{:S(2)}, u32[]{:S(2)}) async-start(f32[6,32,256]{2,0,1:T(8,128)} %broadcast_select_fusion), calls=%async_computation.1 | async-start | bytes 524288 | tf_op jit(solution)/shard_map/all_to_all | solution.py:119
  109.7 6.4 %collective-permute-start.3 = (f32[4,38,3,128]{3,2,1,0:T(4,128)S(1)}, f32[4,38,3,128]{3,2,1,0:T(4,128)S(1)}, u32[]{:S(2)}, u32[]{:S(2)}) collective-permute-start(f32[4,38,3,128]{3,2,1,0:T(4,128)S(1)} %get-tuple-element.25), channel_id=1, source_target_pairs={{1,0},{2,1},{3,2},{5,4},{6,5},{7,6},{9,8},{10,9},{11,10},{13,12},{... | collective-permute-start | bytes 700424 | tf_op jit(solution)/shard_map/ppermute | solution.py:21
  111.0 5.1 %collective-permute-start.2 = (f32[4,38,3,128]{3,2,1,0:T(4,128)S(1)}, f32[4,38,3,128]{3,2,1,0:T(4,128)S(1)}, u32[]{:S(2)}, u32[]{:S(2)}) collective-permute-start(f32[4,38,3,128]{3,2,1,0:T(4,128)S(1)} %get-tuple-element.24), channel_id=1, source_target_pairs={{0,1},{1,2},{2,3},{4,5},{5,6},{6,7},{8,9},{9,10},{10,11},{12,13},{... | collective-permute-start | bytes 700424 | tf_op jit(solution)/shard_map/ppermute | solution.py:20
  118.3 2.6 %copy-start.9 = (s32[4096]{0:T(1024)S(1)}, s32[4096]{0:T(1024)}, u32[]{:S(2)}) copy-start(s32[4096]{0:T(1024)} %broadcast_clamp_fusion.1) | copy-start | bytes 49156
  137.3 7.9 %copy-start.3 = (f32[1,32,32,128]{3,2,1,0:T(8,128)S(1)}, f32[1,32,32,128]{3,2,1,0:T(8,128)}, u32[]{:S(2)}) copy-start(f32[1,32,32,128]{3,2,1,0:T(8,128)} %get-tuple-element.28) | copy-start | bytes 1572868
  137.3 7.9 %copy-start.15 = (s32[128]{0:T(128)S(1)}, s32[128]{0:T(128)}, u32[]{:S(2)}) copy-start(s32[128]{0:T(128)} %copy-done.14) | copy-start | bytes 1540
  137.4 7.9 %copy-start.17 = (pred[128]{0:T(512)(128)(4,1)S(1)}, pred[128]{0:T(512)(128)(4,1)}, u32[]{:S(2)}) copy-start(pred[128]{0:T(512)(128)(4,1)} %copy-done.16) | copy-start | bytes 388
  137.4 8.0 %copy-start.18 = (f32[128]{0:T(128)S(1)}, f32[128]{0:T(128)}, u32[]{:S(2)}) copy-start(f32[128]{0:T(128)} %broadcast_multiply_fusion.2) | copy-start | bytes 1540
  144.9 4.0 %copy-start.2 = (f32[1024,128]{1,0:T(8,128)S(1)}, f32[1024,128]{1,0:T(8,128)}, u32[]{:S(2)}) copy-start(f32[1024,128]{1,0:T(8,128)} %copy.87) | copy-start | bytes 1572868
  151.4 2.1 copy-start.13
  151.9 1.3 copy-start.1
  172.4 16.9 %all-to-all-start.2 = ((f32[3,32,256]{2,0,1:T(4,128)}), f32[3,32,256]{2,0,1:T(4,128)S(1)}, u32[]{:S(2)}, u32[]{:S(2)}) async-start(f32[3,32,256]{2,0,1:T(4,128)} %copy.90), calls=%async_computation.2 | async-start | bytes 262144 | tf_op jit(solution)/shard_map/all_to_all | solution.py:135
  182.4 72.2 %collective-permute-start.7 = (f32[3,130,1]{2,1,0:T(8,128)S(1)}, f32[3,130,1]{2,1,0:T(8,128)S(1)}, u32[]{:S(2)}, u32[]{:S(2)}) collective-permute-start(f32[3,130,1]{2,1,0:T(8,128)S(1)} %get-tuple-element.36), channel_id=1, source_target_pairs={{0,1},{1,2},{2,3},{4,5},{5,6},{6,7},{8,9},{9,10},{10,11},{12,13},{... | collective-permute-start | bytes 4688 | tf_op jit(solution)/shard_map/ppermute | solution.py:20
  184.4 70.2 %collective-permute-start.6 = (f32[3,130,1]{2,1,0:T(8,128)S(1)}, f32[3,130,1]{2,1,0:T(8,128)S(1)}, u32[]{:S(2)}, u32[]{:S(2)}) collective-permute-start(f32[3,130,1]{2,1,0:T(8,128)S(1)} %get-tuple-element.35), channel_id=1, source_target_pairs={{1,0},{2,1},{3,2},{5,4},{6,5},{7,6},{9,8},{10,9},{11,10},{13,12},{... | collective-permute-start | bytes 4688 | tf_op jit(solution)/shard_map/ppermute | solution.py:21
  249.3 5.3 %copy-start.6 = (f32[3,128,128]{2,1,0:T(8,128)S(1)}, f32[3,128,128]{2,1,0:T(8,128)}, u32[]{:S(2)}) copy-start(f32[3,128,128]{2,1,0:T(8,128)} %param.9) | copy-start | bytes 589828
where the time goes:
time: 258 us; the launch traced here: 256 us
  other arithmetic  104 us (40%)
  local copies, waits for them, and re-layouts  104 us (40%)
  starting transfers between devices  41.3 us (16%)
  waiting for transfers between devices  2.85 us (1%)
    scatter-add x1, other arithmetic, body(): shell_force = jnp.zeros((3, rows_x * rows_y), jnp.float32).at[:, asked_no...  57.3 us
    gather x2, local copies, waits for them, and re-layouts, body(): picked = jnp.take(stacked, asked_nodes, axis=1)  34.1 us
    gather x1, local copies, waits for them, and re-layouts, body(): motion = jnp.take(replies, slot_index, axis=1).reshape(6, points, stencil)  16.4 us
    scatter x1, local copies, waits for them, and re-layouts, body(): jnp.zeros((devices * capacity,), jnp.int32).at[slot_index].set(node_ids)  16.1 us
    scatter x1, other arithmetic, body(): jnp.zeros((3, devices * capacity), jnp.float32).at[:, slot_index]  14.9 us
    ppermute x4, starting transfers between devices, with_halo(): before = lax.ppermute(last, axis, up)  11.5 us
    all_to_all x1, starting transfers between devices, body(): lax.all_to_all(outgoing, ('span', 'chord'), split_axis=1, concat_axis=1,...  9.79 us
    another operation x3, other arithmetic  9.62 us
  transfers between devices with their start and end apart: 11, of which 1 were waited for; matrix products, arithmetic and copies ran while one was open for 49% of the time, Pallas kernels for 0%

commit v1 on v0

--- a/solution.py
+++ b/solution.py
@@ -132,7 +132,15 @@
     surface_load = normals * pressure[None]
     contrib = (surface_load[:, :, None] * rbf_weight[None]).reshape(3, -1)
     outgoing = jnp.zeros((3, devices * capacity), jnp.float32).at[:, slot_index].set(contrib)
-    arrived = lax.all_to_all(outgoing, ("span", "chord"), split_axis=1, concat_axis=1, tiled=True)
+    arrived = jnp.concatenate(
+        lax.all_to_all(
+            jnp.stack(jnp.split(outgoing, lax.axis_size(("span", "chord")), axis=1)),
+            ("span", "chord"),
+            0,
+            0,
+        ),
+        axis=1,
+    )
     shell_force = (
         jnp.zeros((3, rows_x * rows_y), jnp.float32)
         .at[:, asked_nodes]

time: 258 us -> 315 us (1.22)
  local copies, waits for them, and re-layouts: 104 us -> 157 us
    unnamed x44 -> x63, local copies, waits for them, and re-layouts: 5.4 us -> 55.3 us
    all_to_all x2 -> x0, local copies, waits for them, and re-layouts: 6.09 us -> none  [body(): lax.all_to_all(outgoing, ('span', 'chord'), split_axis=1, concat_axis=1,...]
    another operation x0 -> x2, local copies, waits for them, and re-layouts: none -> 5.06 us  [body(): jnp.stack(jnp.split(outgoing, lax.axis_size(('span', 'chord')), axis=1))]
  transfers between devices with their start and end apart: 11 -> 11, of which waited for: 1 -> 1; matrix products, arithmetic and copies ran while one was open for 49% -> 40% of each run, Pallas kernels for 0% -> 0%
where the time goes in v1:
time: 315 us; the launch traced here: 313 us
  local copies, waits for them, and re-layouts  157 us (50%)
  other arithmetic  107 us (34%)
  starting transfers between devices  41.4 us (13%)
  matrix products  3.27 us (1%)
    scatter-add x1, other arithmetic, body(): shell_force = jnp.zeros((3, rows_x * rows_y), jnp.float32).at[:, asked_no...  57.3 us
    unnamed x63, local copies, waits for them, and re-layouts  55.3 us
    gather x2, local copies, waits for them, and re-layouts, body(): picked = jnp.take(stacked, asked_nodes, axis=1)  34.1 us
    gather x1, local copies, waits for them, and re-layouts, body(): motion = jnp.take(replies, slot_index, axis=1).reshape(6, points, stencil)  16.4 us
    scatter x1, local copies, waits for them, and re-layouts, body(): jnp.zeros((devices * capacity,), jnp.int32).at[slot_index].set(node_ids)  16.3 us
    scatter x1, other arithmetic, body(): jnp.zeros((3, devices * capacity), jnp.float32).at[:, slot_index]  14.9 us
    ppermute x4, starting transfers between devices, with_halo(): before = lax.ppermute(last, axis, up)  11.3 us
    another operation x3, other arithmetic  10.9 us
  transfers between devices with their start and end apart: 11, of which 1 were waited for; matrix products, arithmetic and copies ran while one was open for 40% of the time, Pallas kernels for 0%

profile of v1, /device:TPU:8, one launch (start us, length us, event | category | flops | bytes accessed | tf_op | source)
XLA Modules:
  0.0 312.8 jit_solution(16413506040312418387)
XLA Ops:
  4.9 9.2 %reduce-window.6 = s32[32,32,128]{2,1,0:T(8,128)S(1)} reduce-window(s32[32,32,128]{2,1,0:T(8,128)S(1)} %fusion.25, s32[]{:T(128)} %constant.34.clone.1), window={size=1x1x128 pad=0_0x0_0x127_0}, to_apply=%region_0.0 | reduce-window | flops 16646144 | bytes 1048580 | tf_op jit(solution)/shard_map/reduce-window
  20.9 16.3 %scatter_custom_fusion = s32[8192]{0:T(1024)} fusion(s32[4096]{0:T(1024)S(1)} %bitcast.201, s32[4096]{0:T(1024)} %reshape.179, s32[]{:T(128)} %constant.34.clone.1), kind=kCustom, calls=%fused_computation.188 | custom fusion | bytes 33280 | tf_op jit(solution)/shard_map/scatter | solution.py:112
  37.2 6.1 %all-to-all-start = ((s32[32,256,1]{1,2,0:T(1,128)}), s32[32,256,1]{1,2,0:T(1,128)}, u32[]{:S(2)}, u32[]{:S(2)}) async-start(s32[32,256,1]{1,2,0:T(1,128)} %bitcast.5), calls=%async_computation | async-start | bytes 65536 | tf_op jit(solution)/shard_map/all_to_all | solution.py:113
  44.1 3.4 %collective-permute-start.1 = (f32[4,3,32,128]{3,2,1,0:T(8,128)}, f32[4,3,32,128]{3,2,1,0:T(8,128)}, u32[]{:S(2)}, u32[]{:S(2)}) collective-permute-start(f32[4,3,32,128]{3,2,1,0:T(8,128)} %get-tuple-element.34), channel_id=1, source_target_pairs={{0,4},{4,8},{8,12},{12,16},{16,20},{20,24},{24,28},{1,5},{5,9},{9,... | collective-permute-start | bytes 589832 | tf_op jit(solution)/shard_map/ppermute | solution.py:20
  47.5 3.4 %collective-permute-start = (f32[4,3,32,128]{3,2,1,0:T(8,128)}, f32[4,3,32,128]{3,2,1,0:T(8,128)}, u32[]{:S(2)}, u32[]{:S(2)}) collective-permute-start(f32[4,3,32,128]{3,2,1,0:T(8,128)} %get-tuple-element.33), channel_id=1, source_target_pairs={{4,0},{8,4},{12,8},{16,12},{20,16},{24,20},{28,24},{5,1},{9,5},{13... | collective-permute-start | bytes 589832 | tf_op jit(solution)/shard_map/ppermute | solution.py:21
  51.4 3.1 collective-permute-start.4
  54.6 2.7 collective-permute-start.5
  63.1 4.7 %copy.146 = f32[6,128,128]{0,2,1:T(8,128)} copy(f32[6,128,128]{2,1,0:T(8,128)S(1)} %pad_maximum_fusion.1) | data formatting | bytes 786432 | tf_op jit(solution)/shard_map/concatenate | solution.py:117
  72.3 31.2 %gather_fusion = f32[8192,6]{1,0:T(8,128)} fusion(f32[6,16384]{0,1:T(8,128)} %bitcast.186, s32[8192]{0:T(1024)S(1)} %broadcast_clamp_fusion), kind=kCustom, calls=%fused_computation | custom fusion | bytes 425984 | tf_op jit(solution)/shard_map/jit(_take)/gather | solution.py:118
  103.6 2.8 copy.147
  108.0 4.9 %all-to-all-start.1 = ((f32[6,32,256]{2,0,1:T(8,128)}), f32[6,32,256]{2,0,1:T(8,128)S(1)}, u32[]{:S(2)}, u32[]{:S(2)}) async-start(f32[6,32,256]{2,0,1:T(8,128)} %broadcast_select_fusion), calls=%async_computation.1 | async-start | bytes 524288 | tf_op jit(solution)/shard_map/all_to_all | solution.py:119
  117.1 3.2 %collective-permute-start.2 = (f32[4,38,3,128]{3,2,1,0:T(4,128)S(1)}, f32[4,38,3,128]{3,2,1,0:T(4,128)S(1)}, u32[]{:S(2)}, u32[]{:S(2)}) collective-permute-start(f32[4,38,3,128]{3,2,1,0:T(4,128)S(1)} %get-tuple-element.24), channel_id=1, source_target_pairs={{0,1},{1,2},{2,3},{4,5},{5,6},{6,7},{8,9},{9,10},{10,11},{12,13},{... | collective-permute-start | bytes 700424 | tf_op jit(solution)/shard_map/ppermute | solution.py:20
  120.4 1.9 fusion.3
  122.8 1.6 fusion.14
  124.5 2.6 copy.148
  127.1 16.4 %gather_fusion.1 = f32[4096,6]{1,0:T(8,128)} fusion(f32[6,8192]{0,1:T(8,128)} %bitcast.188, s32[4096]{0:T(1024)S(1)} %copy-done.7), kind=kCustom, calls=%fused_computation.1 | custom fusion | bytes 212992 | tf_op jit(solution)/shard_map/jit(_take)/gather | solution.py:120
  143.5 7.5 %multiply_reduce_fusion = f32[6,1024]{0,1:T(8,128)S(1)} fusion(f32[6,1024,4]{0,2,1:T(4,128)} %bitcast.190, f32[1024,4]{1,0:T(8,128)S(1)} %copy.149, pred[1024,4]{1,0:T(8,128)(4,1)} %copy.143), kind=kLoop, calls=%fused_computation.22 | loop fusion | flops 67584 | bytes 143360 | tf_op jit(solution)/shard_map/reduce_sum | solution.py:121
  151.3 2.6 fusion.12
  155.1 2.5 fusion.24
  160.4 14.9 %scatter_custom_fusion.1 = f32[3,8192]{0,1:T(8,128)} fusion(s32[4096]{0:T(1024)} %bitcast.203, f32[3,4096]{0,1:T(8,128)S(1)} %bitcast.187, f32[]{:T(128)} %constant.32.clone.1, f32[4096]{0:T(1024)} %mul.202), kind=kCustom, calls=%fused_computation.18 | custom fusion | flops 12288 | bytes 164352 | tf_op jit(solution)/shard_map/scatter | solution.py:134
  176.8 1.6 fusion.65
  178.4 1.6 fusion.64
  179.9 1.6 fusion.63
  183.1 1.6 fusion.61
  184.6 1.6 fusion.60
  186.2 1.6 fusion.59
  187.8 1.6 fusion.58
  189.4 1.6 fusion.57
  190.9 1.6 fusion.56
  192.5 1.6 fusion.55
  194.1 1.6 fusion.54
  195.7 1.6 fusion.53
  197.3 1.6 fusion.52
  200.4 1.6 fusion.50
  203.5 1.6 fusion.48
  205.1 1.6 fusion.47
  209.8 1.6 fusion.44
  219.1 1.6 fusion.38
  222.3 1.6 fusion.36
  223.9 1.6 fusion.35
  225.5 3.5 %copy.154 = f32[32,3,256]{2,1,0:T(4,128)} copy(f32[32,3,256]{1,2,0:T(8,128)} %fusion.35) | data formatting | bytes 196608 | tf_op jit(solution)/shard_map/stack | solution.py:137
  228.9 9.8 %all-to-all-start.2 = ((f32[32,3,256]{2,1,0:T(4,128)}), f32[32,3,256]{2,1,0:T(4,128)S(1)}, u32[]{:S(2)}, u32[]{:S(2)}) async-start(f32[32,3,256]{2,1,0:T(4,128)} %copy.154), calls=%async_computation.2 | async-start | bytes 262144 | tf_op jit(solution)/shard_map/all_to_all | solution.py:136
  238.9 2.0 collective-permute-start.7
  243.2 2.6 all-to-all-done.2
  245.8 2.6 copy.155
  248.5 57.3 %scatter_custom_fusion.2 = f32[3,16384]{0,1:T(8,128)} fusion(s32[8192]{0:T(1024)} %bitcast.199, f32[8192,3]{1,0:T(8,128)} %copy.155, f32[]{:T(128)} %constant.32.clone.1), kind=kCustom, calls=%fused_computation.5 | custom fusion | flops 24576 | bytes 197120 | tf_op jit(solution)/shard_map/scatter-add | solution.py:147
  305.8 5.3 %copy.156 = f32[3,128,128]{2,1,0:T(8,128)S(1)} copy(f32[3,128,128]{0,2,1:T(8,128)} %bitcast.185) | data formatting | bytes 393216 | tf_op jit(solution)/shard_map/reshape | solution.py:148
  311.1 1.7 multiply_add_fusion
  (102 shorter events, 54.3 us)
Async XLA Ops:
  0.6 42.7 %copy-start = (f32[4,32,32,128]{3,2,1,0:T(8,128)S(1)}, f32[4,32,32,128]{3,2,1,0:T(8,128)}, u32[]{:S(2)}) copy-start(f32[4,32,32,128]{3,2,1,0:T(8,128)} %param.7) | copy-start | bytes 6291460
  1.5 49.3 %copy-start.2 = (f32[3,128,128]{2,1,0:T(8,128)S(1)}, f32[3,128,128]{2,1,0:T(8,128)}, u32[]{:S(2)}) copy-start(f32[3,128,128]{2,1,0:T(8,128)} %param.8) | copy-start | bytes 589828
  14.1 49.0 %copy-start.3 = (f32[3,128,128]{2,1,0:T(8,128)S(1)}, f32[3,128,128]{2,1,0:T(8,128)}, u32[]{:S(2)}) copy-start(f32[3,128,128]{2,1,0:T(8,128)} %param.9) | copy-start | bytes 589828
  19.6 0.6 copy-start.5
  20.9 37.3 %copy-start.8 = (s32[4096,1]{0,1:T(1,128)}, s32[4096,1]{0,1:T(1,128)S(1)}, u32[]{:S(2)}) copy-start(s32[4096,1]{0,1:T(1,128)S(1)} %compare_select_fusion.1) | copy-start | bytes 49156
  37.2 34.3 %all-to-all-start = ((s32[32,256,1]{1,2,0:T(1,128)}), s32[32,256,1]{1,2,0:T(1,128)}, u32[]{:S(2)}, u32[]{:S(2)}) async-start(s32[32,256,1]{1,2,0:T(1,128)} %bitcast.5), calls=%async_computation | async-start | bytes 65536 | tf_op jit(solution)/shard_map/all_to_all | solution.py:113
  44.1 68.8 %collective-permute-start.1 = (f32[4,3,32,128]{3,2,1,0:T(8,128)}, f32[4,3,32,128]{3,2,1,0:T(8,128)}, u32[]{:S(2)}, u32[]{:S(2)}) collective-permute-start(f32[4,3,32,128]{3,2,1,0:T(8,128)} %get-tuple-element.34), channel_id=1, source_target_pairs={{0,4},{4,8},{8,12},{12,16},{16,20},{20,24},{24,28},{1,5},{5,9},{9,... | collective-permute-start | bytes 589832 | tf_op jit(solution)/shard_map/ppermute | solution.py:20
  47.5 67.3 %collective-permute-start = (f32[4,3,32,128]{3,2,1,0:T(8,128)}, f32[4,3,32,128]{3,2,1,0:T(8,128)}, u32[]{:S(2)}, u32[]{:S(2)}) collective-permute-start(f32[4,3,32,128]{3,2,1,0:T(8,128)} %get-tuple-element.33), channel_id=1, source_target_pairs={{4,0},{8,4},{12,8},{16,12},{20,16},{24,20},{28,24},{5,1},{9,5},{13... | collective-permute-start | bytes 589832 | tf_op jit(solution)/shard_map/ppermute | solution.py:21
  51.4 19.4 %collective-permute-start.4 = (f32[3,1,128]{2,1,0:T(1,128)}, f32[3,1,128]{2,1,0:T(1,128)S(1)}, u32[]{:S(2)}, u32[]{:S(2)}) collective-permute-start(f32[3,1,128]{2,1,0:T(1,128)} %get-tuple-element.38), channel_id=1, source_target_pairs={{4,0},{8,4},{12,8},{16,12},{20,16},{24,20},{28,24},{5,1},{9,5},{13... | collective-permute-start | bytes 4616 | tf_op jit(solution)/shard_map/ppermute | solution.py:21
  54.6 16.3 %collective-permute-start.5 = (f32[3,1,128]{2,1,0:T(1,128)}, f32[3,1,128]{2,1,0:T(1,128)}, u32[]{:S(2)}, u32[]{:S(2)}) collective-permute-start(f32[3,1,128]{2,1,0:T(1,128)} %get-tuple-element.37), channel_id=1, source_target_pairs={{0,4},{4,8},{8,12},{12,16},{16,20},{20,24},{24,28},{1,5},{5,9},{9,... | collective-permute-start | bytes 4616 | tf_op jit(solution)/shard_map/ppermute | solution.py:20
  58.2 9.7 %copy-start.11 = (s32[128]{0:T(128)}, s32[128]{0:T(128)S(1)}, u32[]{:S(2)}) copy-start(s32[128]{0:T(128)S(1)} %iota_add_fusion.1) | copy-start | bytes 1540
  58.2 9.7 %copy-start.12 = (pred[128]{0:T(512)(128)(4,1)}, pred[128]{0:T(512)(128)(4,1)S(1)}, u32[]{:S(2)}) copy-start(pred[128]{0:T(512)(128)(4,1)S(1)} %iota_compare_fusion.2) | copy-start | bytes 388
  63.1 4.7 %copy-start.9 = (f32[1024,4]{0,1:T(4,128)S(1)}, f32[1024,4]{0,1:T(4,128)}, u32[]{:S(2)}) copy-start(f32[1024,4]{0,1:T(4,128)} %param.12) | copy-start | bytes 49156
  72.3 31.3 %copy-start.6 = (s32[8192,1]{0,1:T(1,128)}, s32[8192,1]{0,1:T(1,128)S(1)}, u32[]{:S(2)}) copy-start(s32[8192,1]{0,1:T(1,128)S(1)} %compare_select_fusion) | copy-start | bytes 98308
  108.0 16.5 %all-to-all-start.1 = ((f32[6,32,256]{2,0,1:T(8,128)}), f32[6,32,256]{2,0,1:T(8,128)S(1)}, u32[]{:S(2)}, u32[]{:S(2)}) async-start(f32[6,32,256]{2,0,1:T(8,128)} %broadcast_select_fusion), calls=%async_computation.1 | async-start | bytes 524288 | tf_op jit(solution)/shard_map/all_to_all | solution.py:119
  115.8 6.4 %collective-permute-start.3 = (f32[4,38,3,128]{3,2,1,0:T(4,128)S(1)}, f32[4,38,3,128]{3,2,1,0:T(4,128)S(1)}, u32[]{:S(2)}, u32[]{:S(2)}) collective-permute-start(f32[4,38,3,128]{3,2,1,0:T(4,128)S(1)} %get-tuple-element.25), channel_id=1, source_target_pairs={{1,0},{2,1},{3,2},{5,4},{6,5},{7,6},{9,8},{10,9},{11,10},{13,12},{... | collective-permute-start | bytes 700424 | tf_op jit(solution)/shard_map/ppermute | solution.py:21
  117.1 5.1 %collective-permute-start.2 = (f32[4,38,3,128]{3,2,1,0:T(4,128)S(1)}, f32[4,38,3,128]{3,2,1,0:T(4,128)S(1)}, u32[]{:S(2)}, u32[]{:S(2)}) collective-permute-start(f32[4,38,3,128]{3,2,1,0:T(4,128)S(1)} %get-tuple-element.24), channel_id=1, source_target_pairs={{0,1},{1,2},{2,3},{4,5},{5,6},{6,7},{8,9},{9,10},{10,11},{12,13},{... | collective-permute-start | bytes 700424 | tf_op jit(solution)/shard_map/ppermute | solution.py:20
  122.8 4.3 %copy-start.7 = (s32[4096]{0:T(1024)S(1)}, s32[4096]{0:T(1024)}, u32[]{:S(2)}) copy-start(s32[4096]{0:T(1024)} %broadcast_clamp_fusion.1) | copy-start | bytes 49156
  157.6 2.1 copy-start.10
  158.1 1.3 copy-start.1
  228.9 16.9 %all-to-all-start.2 = ((f32[32,3,256]{2,1,0:T(4,128)}), f32[32,3,256]{2,1,0:T(4,128)S(1)}, u32[]{:S(2)}, u32[]{:S(2)}) async-start(f32[32,3,256]{2,1,0:T(4,128)} %copy.154), calls=%async_computation.2 | async-start | bytes 262144 | tf_op jit(solution)/shard_map/all_to_all | solution.py:136
  238.9 72.2 %collective-permute-start.7 = (f32[3,130,1]{2,1,0:T(8,128)S(1)}, f32[3,130,1]{2,1,0:T(8,128)S(1)}, u32[]{:S(2)}, u32[]{:S(2)}) collective-permute-start(f32[3,130,1]{2,1,0:T(8,128)S(1)} %get-tuple-element.36), channel_id=1, source_target_pairs={{0,1},{1,2},{2,3},{4,5},{5,6},{6,7},{8,9},{9,10},{10,11},{12,13},{... | collective-permute-start | bytes 4688 | tf_op jit(solution)/shard_map/ppermute | solution.py:20
  240.9 70.2 %collective-permute-start.6 = (f32[3,130,1]{2,1,0:T(8,128)S(1)}, f32[3,130,1]{2,1,0:T(8,128)S(1)}, u32[]{:S(2)}, u32[]{:S(2)}) collective-permute-start(f32[3,130,1]{2,1,0:T(8,128)S(1)} %get-tuple-element.35), channel_id=1, source_target_pairs={{1,0},{2,1},{3,2},{5,4},{6,5},{7,6},{9,8},{10,9},{11,10},{13,12},{... | collective-permute-start | bytes 4688 | tf_op jit(solution)/shard_map/ppermute | solution.py:21
  305.8 5.3 %copy-start.4 = (f32[3,128,128]{2,1,0:T(8,128)S(1)}, f32[3,128,128]{2,1,0:T(8,128)}, u32[]{:S(2)}) copy-start(f32[3,128,128]{2,1,0:T(8,128)} %param.9) | copy-start | bytes 589828
